TPU v7x, 256 devices: a whole 4x4x8 slice. The times are simulated.
256 devices in a mesh: group: 4 (over x), dp: 16 (over z_lo, y, core), mp: 4 (over z_hi).
Axes of the slice: x: 4, y: 4, z: 8 (z_hi: 4, z_lo: 2; z = z_hi * 2 + z_lo), core: 2. Of those that a mesh axis runs over, the one named last changes fastest.
Arguments:
- block_input: bfloat16 [768, 8192], P(None, 'dp'), may hold values from -6 to 6
- parent_gate_up: bfloat16 [2, 8192, 14336], P(None, 'dp', ('group', 'mp')), may hold values from -0.0625 to 0.0625
- parent_down: bfloat16 [14336, 8192], P(('group', 'mp'), 'dp'), may hold values from -0.046875 to 0.046875
- variant_gate_up: bfloat16 [4, 2, 8192, 3584], P('group', None, 'dp', 'mp'), may hold values from -0.0625 to 0.0625
- variant_down: bfloat16 [4, 3584, 8192], P('group', 'mp', 'dp'), may hold values from -0.09375 to 0.09375
- widths: int32 [4], P('group'), may hold values from 896 to 3584, as said below
Outputs:
- grad_gate_up: float32 [4, 2, 8192, 3584], P('group', None, 'dp', 'mp')
- grad_down: float32 [4, 3584, 8192], P('group', 'mp', 'dp')
Inputs may be any that keep to these rules, and one draw needn't show every extreme that they name: Variant v uses its hidden units 0 to widths[v] - 1; one variant uses all 3584 of them and another exactly a quarter of 3584.
All inputs are finite; a program needn't handle non-finite values.
Results may differ from a plain program's by a relative error of at most 0.008.
Values may be sent and summed in bfloat16 or wider, within the bound.
No kernel may reach another device: no remote copies, remote signals or barrier semaphores. Data moves between devices by JAX's collectives and lax.ppermute only.
A program may use at most 64 MiB of HBM per device.

v0:
```python
import math
import jax
import jax.numpy as jnp
from jax import lax
from jax.sharding import PartitionSpec as P


def gated_values(pre_act, unit_mask):
    gate_value = pre_act[:, 0].astype(jnp.float32)
    up_value = pre_act[:, 1].astype(jnp.float32)
    sigmoid_gate = jax.nn.sigmoid(gate_value)
    return (gate_value * sigmoid_gate * up_value * unit_mask).astype(jnp.bfloat16)


def pre_gradient(pre_act, unit_mask, hidden_grad):
    gate_value = pre_act[:, 0].astype(jnp.float32)
    up_value = pre_act[:, 1].astype(jnp.float32)
    sigmoid_gate = jax.nn.sigmoid(gate_value)
    masked_grad = hidden_grad * unit_mask
    grad_gate = masked_grad * up_value * sigmoid_gate * (1.0 + gate_value * (1.0 - sigmoid_gate))
    grad_up = masked_grad * gate_value * sigmoid_gate
    return jnp.stack([grad_gate, grad_up], axis=1).astype(jnp.bfloat16)


def body(block_input, parent_gate_up, parent_down, variant_gate_up, variant_down, widths):
    local_gate_up = variant_gate_up[0]
    local_down = variant_down[0]
    local_units = local_down.shape[0]
    all_tokens = block_input.shape[0]
    first_unit = lax.axis_index("mp") * local_units
    unit_index = first_unit + jnp.arange(local_units, dtype=jnp.int32)
    unit_mask = (unit_index < widths[0]).astype(jnp.float32)
    parent_term = jnp.einsum(
        "td,kdf->tkf", block_input, parent_gate_up, preferred_element_type=jnp.float32
    )
    variant_term = jnp.einsum(
        "td,kdf->tkf", block_input, local_gate_up, preferred_element_type=jnp.float32
    )
    parent_rows, variant_rows = (
        lax.psum_scatter(parent_term, "dp", scatter_dimension=0, tiled=True),
        lax.psum_scatter(variant_term, "dp", scatter_dimension=0, tiled=True),
    )
    parent_pre = parent_rows.astype(jnp.bfloat16)
    variant_pre = variant_rows.astype(jnp.bfloat16)
    parent_hidden = gated_values(parent_pre, 1.0)
    parent_all, variant_all = (
        lax.all_gather(parent_hidden, "dp", axis=0, tiled=True),
        lax.all_gather(variant_pre, "dp", axis=0, tiled=True),
    )
    variant_hidden = gated_values(variant_all, unit_mask)
    teacher_part = jnp.dot(parent_all, parent_down, preferred_element_type=jnp.float32)
    student_part = jnp.dot(variant_hidden, local_down, preferred_element_type=jnp.float32)
    teacher = lax.psum(teacher_part, ("group", "mp"))
    student = lax.psum(student_part, "mp")
    loss_scale = 1.0 / math.sqrt(all_tokens)
    output_grad = ((student - teacher) * loss_scale).astype(jnp.bfloat16)
    grad_down = lax.dot_general(
        variant_hidden, output_grad, (((0,), (0,)), ((), ())), preferred_element_type=jnp.float32
    )
    hidden_part = lax.dot_general(
        output_grad, local_down, (((1,), (1,)), ((), ())), preferred_element_type=jnp.float32
    )
    hidden_full = lax.psum(hidden_part, "dp")
    grad_pre = pre_gradient(variant_all, unit_mask, hidden_full)
    grad_gate_up = jnp.einsum(
        "td,tkf->kdf", block_input, grad_pre, preferred_element_type=jnp.float32
    )
    return (grad_gate_up[None], grad_down[None])


def solution(mesh):
    in_specs = (
        P(None, "dp"),
        P(None, "dp", ("group", "mp")),
        P(("group", "mp"), "dp"),
        P("group", None, "dp", "mp"),
        P("group", "mp", "dp"),
        P("group"),
    )
    out_specs = (P("group", None, "dp", "mp"), P("group", "mp", "dp"))
    return jax.shard_map(body, mesh=mesh, in_specs=in_specs, out_specs=out_specs, check_vma=False)
```

profile of v0, /device:TPU:1, one launch (start us, length us, event | category | flops | bytes accessed | tf_op | source)
XLA Modules:
  0.0 652.1 jit_solution(2625803845936884595)
XLA Ops:
  7.2 0.0 copy-start
  7.2 0.0 reduce-scatter.5.cloned.1.call-start
  7.2 1.4 copy-done
  8.7 5.2 fusion.45
  13.9 0.0 copy-start.1
  13.9 0.0 reduce-scatter.5.cloned.1.call-update
  13.9 0.0 reduce-scatter.3.cloned.1.call-start
  13.9 1.1 copy-done.1
  15.0 5.5 fusion.29
  20.5 0.0 reduce-scatter.3.cloned.1.call-update
  20.5 0.0 all-gather.5.cloned.1.call-start
  20.6 66.0 %reduce-scatter.5.cloned.1.call-done = f32[48,2,896]{2,0,1:T(8,128)} async-done(((f32[768,2,896]{2,0,1:T(8,128)}), f32[48,2,896]{2,0,1:T(8,128)}) %reduce-scatter.5.cloned.1.call-update) | async-done | bytes 344080 | tf_op jit(solution)/shard_map/reduce_scatter | solution.py:40
  86.6 1.0 convert_element_type.66
  87.6 0.7 fusion.52
  88.3 0.0 all-gather.5.cloned.1.call-update
  88.3 0.0 all-gather.3.cloned.1.call-start
  88.4 71.3 %reduce-scatter.3.cloned.1.call-done = f32[48,2,896]{2,0,1:T(8,128)} async-done(((f32[768,2,896]{2,0,1:T(8,128)}), f32[48,2,896]{2,0,1:T(8,128)}) %reduce-scatter.3.cloned.1.call-update) | async-done | bytes 344080 | tf_op jit(solution)/shard_map/reduce_scatter | solution.py:41
  159.7 1.7 convert_element_type.60
  161.3 0.0 all-gather.3.cloned.1.call-update
  161.3 0.0 copy-start.2
  161.4 0.0 all-reduce.6.cloned.1.call-start
  161.4 38.0 %all-gather.5.cloned.1.call-done = bf16[768,896]{1,0:T(8,128)(2,1)} async-done(((bf16[48,896]{1,0:T(8,128)(2,1)}), bf16[768,896]{1,0:T(8,128)(2,1)}) %all-gather.5.cloned.1.call-update) | async-done | bytes 1376272 | tf_op jit(solution)/shard_map/all_gather | solution.py:47
  199.4 3.7 fusion.57
  203.1 0.0 all-reduce.6.cloned.1.call-update
  203.1 0.0 all-reduce.4.cloned.1.call-start
  203.8 35.3 %all-gather.3.cloned.1.call-done = bf16[768,2,896]{2,0,1:T(8,128)(2,1)} async-done(((bf16[48,2,896]{2,0,1:T(8,128)(2,1)}), bf16[768,2,896]{2,0,1:T(8,128)(2,1)}) %all-gather.3.cloned.1.call-update) | async-done | bytes 2752528 | tf_op jit(solution)/shard_map/all_gather | solution.py:48
  239.1 0.0 copy-done.2
  239.1 4.0 fusion.31
  243.2 0.0 all-reduce.4.cloned.1.call-update
  243.2 0.0 all-reduce.8.cloned.1.call-start
  243.2 163.2 %all-reduce.6.cloned.1.call-done = f32[768,512]{1,0:T(8,128)} async-done(((f32[768,512]{1,0:T(8,128)}), f32[768,512]{1,0:T(8,128)}) %all-reduce.6.cloned.1.call-update) | async-done | bytes 1572880 | tf_op jit(solution)/shard_map/psum | solution.py:53
  406.4 93.0 %all-reduce.4.cloned.1.call-done = f32[768,512]{1,0:T(8,128)} async-done(((f32[768,512]{1,0:T(8,128)}), f32[768,512]{1,0:T(8,128)}) %all-reduce.4.cloned.1.call-update) | async-done | bytes 1572880 | tf_op jit(solution)/shard_map/psum | solution.py:54
  499.4 2.3 multiply_convert_fusion
  501.7 3.7 fusion.39
  505.4 0.0 all-reduce.8.cloned.1.call-update
  505.5 4.1 convolution_bitcast_fusion
  509.6 123.6 %all-reduce.8.cloned.1.call-done = f32[768,896]{1,0:T(8,128)} async-done(((f32[768,896]{1,0:T(8,128)}), f32[768,896]{1,0:T(8,128)}) %all-reduce.8.cloned.1.call-update) | async-done | bytes 2752528 | tf_op jit(solution)/shard_map/psum | solution.py:63
  633.2 4.0 fusion.36
  637.2 3.5 fusion.26
  640.7 4.6 copy.9
  (1 shorter events, 0.0 us)
Async XLA Ops:
  7.2 1.5 copy-start
  7.2 79.4 %reduce-scatter.5.cloned.1.call-start = ((), (), s32[]{:S(2)}) async-start(), calls=%async_computation.5 | async-start | bytes 5849088 | tf_op jit(solution)/shard_map/reduce_scatter | solution.py:40
  13.9 1.1 copy-start.1
  13.9 145.8 %reduce-scatter.3.cloned.1.call-start = ((), (), s32[]{:S(2)}) async-start(), calls=%async_computation.2 | async-start | bytes 5849088 | tf_op jit(solution)/shard_map/reduce_scatter | solution.py:41
  20.5 178.9 %all-gather.5.cloned.1.call-start = ((), (), s32[]{:S(2)}) async-start(), calls=%async_computation.6 | async-start | bytes 1462272 | tf_op jit(solution)/shard_map/all_gather | solution.py:47
  88.3 150.8 %all-gather.3.cloned.1.call-start = ((), (), s32[]{:S(2)}) async-start(), calls=%async_computation.3 | async-start | bytes 2924544 | tf_op jit(solution)/shard_map/all_gather | solution.py:48
  161.3 77.8 %copy-start.2 = (bf16[1,896,512]{2,1,0:T(8,128)(2,1)S(1)}, bf16[1,896,512]{2,1,0:T(8,128)(2,1)}, u32[]{:S(2)}) copy-start(bf16[1,896,512]{2,1,0:T(8,128)(2,1)} %param.10) | copy-start | bytes 2752516
  161.4 245.1 %all-reduce.6.cloned.1.call-start = ((), (), s32[]{:S(2)}) async-start(), calls=%async_computation.7 | async-start | bytes 3145728 | tf_op jit(solution)/shard_map/psum | solution.py:53
  203.1 296.3 %all-reduce.4.cloned.1.call-start = ((), (), s32[]{:S(2)}) async-start(), calls=%async_computation.4 | async-start | bytes 3145728 | tf_op jit(solution)/shard_map/psum | solution.py:54
  243.2 390.0 %all-reduce.8.cloned.1.call-start = ((), (), s32[]{:S(2)}) async-start(), calls=%async_computation.8 | async-start | bytes 5505024 | tf_op jit(solution)/shard_map/psum | solution.py:63
Sparse Core Ops, SparseCore 0:
  14.0 72.5 reduce-scatter.4
  89.1 70.4 reduce-scatter.2
  162.1 37.2 all-gather.4
  201.6 37.4 all-gather.2
  242.2 164.1 all-reduce.5
  409.5 89.8 all-reduce.3
  505.6 127.5 all-reduce.7
where the time goes:
time: 653 us; the launch traced here: 652 us
  waiting for transfers between devices  590 us (90%)
  matrix products  29.8 us (5%)
  between operations  14.8 us (2%)
  other arithmetic  9.67 us (1%)
  local copies, waits for them, and re-layouts  7.1 us (1%)
    psum x1, waiting for transfers between devices, body(): teacher = lax.psum(teacher_part, ('group', 'mp'))  163 us
    psum x1, waiting for transfers between devices, body(): hidden_full = lax.psum(hidden_part, 'dp')  124 us
    psum x1, waiting for transfers between devices, body(): student = lax.psum(student_part, 'mp')  93 us
    reduce_scatter x1, waiting for transfers between devices, body(): lax.psum_scatter(variant_term, 'dp', scatter_dimension=0, tiled=True)  71.3 us
    reduce_scatter x1, waiting for transfers between devices, body(): lax.psum_scatter(parent_term, 'dp', scatter_dimension=0, tiled=True)  66 us
    all_gather x1, waiting for transfers between devices, body(): lax.all_gather(parent_hidden, 'dp', axis=0, tiled=True)  38 us
    all_gather x1, waiting for transfers between devices, body(): lax.all_gather(variant_pre, 'dp', axis=0, tiled=True)  35.3 us
  transfers between devices with their start and end apart: 7, of which 7 were waited for; matrix products, arithmetic and copies ran while one was open for 3% of the time, Pallas kernels for 0%

commit v1 on v0

--- a/solution.py
+++ b/solution.py
@@ -50,7 +50,7 @@
     variant_hidden = gated_values(variant_all, unit_mask)
     teacher_part = jnp.dot(parent_all, parent_down, preferred_element_type=jnp.float32)
     student_part = jnp.dot(variant_hidden, local_down, preferred_element_type=jnp.float32)
-    teacher = lax.psum(teacher_part, ("group", "mp"))
+    teacher = lax.psum(lax.psum(teacher_part, "mp"), "group")
     student = lax.psum(student_part, "mp")
     loss_scale = 1.0 / math.sqrt(all_tokens)
     output_grad = ((student - teacher) * loss_scale).astype(jnp.bfloat16)

time: 653 us -> 588 us (0.900)
  waiting for transfers between devices: 590 us -> 526 us
    psum x1, waiting for transfers between devices: 163 us -> 62.3 us  [body(): teacher = lax.psum(lax.psum(teacher_part, 'mp'), 'group')]
    psum x1, waiting for transfers between devices: 93 us -> 127 us  [body(): student = lax.psum(student_part, 'mp')]
where the time goes in v1:
time: 588 us; the launch traced here: 587 us
  waiting for transfers between devices  526 us (89%)
  matrix products  29.7 us (5%)
  between operations  14.8 us (3%)
  other arithmetic  9.67 us (2%)
  local copies, waits for them, and re-layouts  7.1 us (1%)
    psum x1, waiting for transfers between devices, body(): student = lax.psum(student_part, 'mp')  127 us
    psum x1, waiting for transfers between devices, body(): hidden_full = lax.psum(hidden_part, 'dp')  126 us
    reduce_scatter x1, waiting for transfers between devices, body(): lax.psum_scatter(variant_term, 'dp', scatter_dimension=0, tiled=True)  71.3 us
    reduce_scatter x1, waiting for transfers between devices, body(): lax.psum_scatter(parent_term, 'dp', scatter_dimension=0, tiled=True)  66 us
    psum x1, waiting for transfers between devices, body(): teacher = lax.psum(lax.psum(teacher_part, 'mp'), 'group')  62.3 us
    all_gather x1, waiting for transfers between devices, body(): lax.all_gather(parent_hidden, 'dp', axis=0, tiled=True)  37.3 us
    all_gather x1, waiting for transfers between devices, body(): lax.all_gather(variant_pre, 'dp', axis=0, tiled=True)  36 us
  transfers between devices with their start and end apart: 7, of which 7 were waited for; matrix products, arithmetic and copies ran while one was open for 3% of the time, Pallas kernels for 0%

profile of v1, /device:TPU:1, one launch (start us, length us, event | category | flops | bytes accessed | tf_op | source)
XLA Modules:
  0.0 587.2 jit_solution(13210467571178630727)
XLA Ops:
  7.2 0.0 copy-start
  7.2 0.0 reduce-scatter.5.cloned.1.call-start
  7.2 1.4 copy-done
  8.7 5.2 fusion.45
  13.9 0.0 copy-start.1
  13.9 0.0 reduce-scatter.5.cloned.1.call-update
  13.9 0.0 reduce-scatter.3.cloned.1.call-start
  13.9 1.1 copy-done.1
  15.0 5.5 fusion.29
  20.5 0.0 reduce-scatter.3.cloned.1.call-update
  20.5 0.0 all-gather.5.cloned.1.call-start
  20.6 66.0 %reduce-scatter.5.cloned.1.call-done = f32[48,2,896]{2,0,1:T(8,128)} async-done(((f32[768,2,896]{2,0,1:T(8,128)}), f32[48,2,896]{2,0,1:T(8,128)}) %reduce-scatter.5.cloned.1.call-update) | async-done | bytes 344080 | tf_op jit(solution)/shard_map/reduce_scatter | solution.py:40
  86.6 1.0 convert_element_type.66
  87.6 0.7 fusion.52
  88.3 0.0 all-gather.5.cloned.1.call-update
  88.3 0.0 all-gather.3.cloned.1.call-start
  88.4 71.3 %reduce-scatter.3.cloned.1.call-done = f32[48,2,896]{2,0,1:T(8,128)} async-done(((f32[768,2,896]{2,0,1:T(8,128)}), f32[48,2,896]{2,0,1:T(8,128)}) %reduce-scatter.3.cloned.1.call-update) | async-done | bytes 344080 | tf_op jit(solution)/shard_map/reduce_scatter | solution.py:41
  159.6 1.7 convert_element_type.60
  161.3 0.0 all-gather.3.cloned.1.call-update
  161.3 0.0 all-reduce.9.cloned.1.call-start
  162.0 0.0 copy-start.2
  162.1 37.3 %all-gather.5.cloned.1.call-done = bf16[768,896]{1,0:T(8,128)(2,1)} async-done(((bf16[48,896]{1,0:T(8,128)(2,1)}), bf16[768,896]{1,0:T(8,128)(2,1)}) %all-gather.5.cloned.1.call-update) | async-done | bytes 1376272 | tf_op jit(solution)/shard_map/all_gather | solution.py:47
  199.4 3.7 fusion.57
  203.1 36.0 %all-gather.3.cloned.1.call-done = bf16[768,2,896]{2,0,1:T(8,128)(2,1)} async-done(((bf16[48,2,896]{2,0,1:T(8,128)(2,1)}), bf16[768,2,896]{2,0,1:T(8,128)(2,1)}) %all-gather.3.cloned.1.call-update) | async-done | bytes 2752528 | tf_op jit(solution)/shard_map/all_gather | solution.py:48
  239.1 0.0 copy-done.2
  239.1 4.0 fusion.31
  243.1 0.0 all-reduce.9.cloned.1.call-update
  243.1 0.0 all-reduce.5.cloned.1.call-start
  243.2 127.0 %all-reduce.9.cloned.1.call-done = (f32[768,512]{1,0:T(8,128)}, f32[768,512]{1,0:T(8,128)}) async-done(((f32[768,512]{1,0:T(8,128)}, f32[768,512]{1,0:T(8,128)}), (f32[768,512]{1,0:T(8,128)}, f32[768,512]{1,0:T(8,128)})) %all-reduce.9.cloned.1.call-update) | async-done | bytes 3145744 | tf_op jit(solution)/shard_map/psum | solution.py:54
  370.2 0.0 all-reduce.5.cloned.1.call-update
  370.2 0.0 all-reduce.7.cloned.1.call-start
  370.2 62.3 %all-reduce.5.cloned.1.call-done = f32[768,512]{1,0:T(8,128)} async-done(((f32[768,512]{1,0:T(8,128)}), f32[768,512]{1,0:T(8,128)}) %all-reduce.5.cloned.1.call-update) | async-done | bytes 1572880 | tf_op jit(solution)/shard_map/psum | solution.py:53
  432.6 2.3 multiply_convert_fusion
  434.9 3.7 fusion.39
  438.6 0.0 all-reduce.7.cloned.1.call-update
  438.6 4.1 convolution_bitcast_fusion
  442.7 125.6 %all-reduce.7.cloned.1.call-done = f32[768,896]{1,0:T(8,128)} async-done(((f32[768,896]{1,0:T(8,128)}), f32[768,896]{1,0:T(8,128)}) %all-reduce.7.cloned.1.call-update) | async-done | bytes 2752528 | tf_op jit(solution)/shard_map/psum | solution.py:63
  568.3 4.0 fusion.36
  572.3 3.4 fusion.26
  575.8 4.6 copy.9
  (1 shorter events, 0.0 us)
Async XLA Ops:
  7.2 1.5 copy-start
  7.2 79.4 %reduce-scatter.5.cloned.1.call-start = ((), (), s32[]{:S(2)}) async-start(), calls=%async_computation.4 | async-start | bytes 5849088 | tf_op jit(solution)/shard_map/reduce_scatter | solution.py:40
  13.9 1.1 copy-start.1
  13.9 145.8 %reduce-scatter.3.cloned.1.call-start = ((), (), s32[]{:S(2)}) async-start(), calls=%async_computation.2 | async-start | bytes 5849088 | tf_op jit(solution)/shard_map/reduce_scatter | solution.py:41
  20.5 178.9 %all-gather.5.cloned.1.call-start = ((), (), s32[]{:S(2)}) async-start(), calls=%async_computation.5 | async-start | bytes 1462272 | tf_op jit(solution)/shard_map/all_gather | solution.py:47
  88.3 150.8 %all-gather.3.cloned.1.call-start = ((), (), s32[]{:S(2)}) async-start(), calls=%async_computation.3 | async-start | bytes 2924544 | tf_op jit(solution)/shard_map/all_gather | solution.py:48
  161.3 208.8 %all-reduce.9.cloned.1.call-start = ((), (), s32[]{:S(2)}) async-start(), calls=%async_computation.8 | async-start | bytes 6291456 | tf_op jit(solution)/shard_map/psum | solution.py:54
  162.0 77.1 %copy-start.2 = (bf16[1,896,512]{2,1,0:T(8,128)(2,1)S(1)}, bf16[1,896,512]{2,1,0:T(8,128)(2,1)}, u32[]{:S(2)}) copy-start(bf16[1,896,512]{2,1,0:T(8,128)(2,1)} %param.10) | copy-start | bytes 2752516
  243.1 189.4 %all-reduce.5.cloned.1.call-start = ((), (), s32[]{:S(2)}) async-start(), calls=%async_computation.6 | async-start | bytes 3145728 | tf_op jit(solution)/shard_map/psum | solution.py:53
  370.2 198.1 %all-reduce.7.cloned.1.call-start = ((), (), s32[]{:S(2)}) async-start(), calls=%async_computation.7 | async-start | bytes 5505024 | tf_op jit(solution)/shard_map/psum | solution.py:63
Sparse Core Ops, SparseCore 0:
  14.0 72.5 reduce-scatter.4
  89.1 70.4 reduce-scatter.2
  162.1 37.2 all-gather.4
  201.6 37.4 all-gather.2
  243.3 126.8 all-reduce.8
  372.4 60.1 all-reduce.4
  438.7 129.5 all-reduce.6
